TPU v7x, 32 devices: a whole 2x2x4 slice. The times are simulated.
32 devices in a mesh: img: 2 (over y), row: 8 (over z, x), col: 2 (over core).
Axes of the slice: x: 2, y: 2, z: 4, core: 2. Of those that a mesh axis runs over, the one named last changes fastest.
Arguments:
- features: bfloat16 [16, 128, 512], P(('img', 'row'), 'col'), parts along dimension 0, may hold values from -60 to 60
- first_gain: float32 [512], replicated, may hold values from 0.1 to 1.9
- first_shift: float32 [512], replicated, may hold values from -2.5 to 2.5
- first_weight: bfloat16 [3, 3, 512, 512], P(None, None, 'row'), may hold values from -0.09375 to 0.09375
- first_bias: float32 [512], replicated, may hold values from -2.5 to 2.5
- second_gain: float32 [512], replicated, may hold values from 0.1 to 1.9
- second_shift: float32 [512], replicated, may hold values from -2.5 to 2.5
- second_weight: bfloat16 [3, 3, 512, 512], P(None, None, 'row'), may hold values from -0.09375 to 0.09375
- second_bias: float32 [512], replicated, may hold values from -2.5 to 2.5
- upsample_weight: bfloat16 [3, 3, 512, 512], P(None, None, 'row'), may hold values from -0.09375 to 0.09375
- upsample_bias: float32 [512], replicated, may hold values from -2.5 to 2.5
Outputs:
- upsampled: bfloat16 [32, 256, 512], P(('img', 'row'), 'col'), parts along dimension 0
There are 2 independent parts, one for each index of `img`. A program takes and returns all parts, laid end to end along the dimension named above; an argument that names none is the same for every part. Nothing has to cross between parts.
All inputs are finite; a program needn't handle non-finite values.
Results may differ from a plain program's by a relative error of at most 0.0075.
Values may be sent and summed in bfloat16 or wider, within the bound.
A program may use at most 128 MiB of HBM per device.

v0:
```python
import jax
import jax.numpy as jnp
from jax import lax
from jax.sharding import PartitionSpec as P

G = 32


EPS = 1e-06


def extended(cells, sides, width):
    for axis, dim in sides:
        count = lax.axis_size(axis)
        ends = count - 1
        head = lax.slice_in_dim(cells, 0, width, axis=dim)
        tail = lax.slice_in_dim(cells, cells.shape[dim] - width, cells.shape[dim], axis=dim)
        cells = jnp.concatenate(
            [
                lax.ppermute(tail, axis, [(i, (i + 1) % count) for i in range(ends)]),
                cells,
                lax.ppermute(head, axis, [((i + 1) % count, i) for i in range(ends)]),
            ],
            axis=dim,
        )
    return cells


def norm_silu(values, gain, shift):
    height, breadth, channels = values.shape
    grouped = values.reshape(height * breadth, G, channels // G)
    total = jnp.sum(grouped, axis=(0, 2))
    squares = jnp.sum(grouped * grouped, axis=(0, 2))
    total, squares = lax.psum((total, squares), ("row", "col"))
    count = height * breadth * lax.axis_size("row") * lax.axis_size("col") * (channels // G)
    mean = total / count
    var = squares / count - mean * mean
    factor = lax.rsqrt(var + EPS)
    normed = (grouped - mean[None, :, None]) * factor[None, :, None]
    normed = normed.reshape(height, breadth, channels) * gain + shift
    return jax.nn.silu(normed).astype(jnp.bfloat16)


def extend(values):
    return extended(values, (("row", 0), ("col", 1)), 1)


def convolve(padded, weight, bias, height, breadth):
    outputs = weight.shape[3]
    empty = jnp.zeros((height, breadth, outputs), jnp.float32)
    share = weight.shape[2] // lax.axis_size("col")
    own = lax.dynamic_slice_in_dim(weight, lax.axis_index("col") * share, share, 2)
    total = empty
    piece = lax.all_gather(own, ("row", "col"), axis=2, tiled=True)
    depth = piece.shape[2]
    offset = jnp.asarray(jnp.int32(0), jnp.int32)
    for offset_y in range(3):
        for offset_x in range(3):
            window = lax.dynamic_slice(
                padded, (jnp.int32(offset_y), jnp.int32(offset_x), offset), (height, breadth, depth)
            )
            total = total + jnp.einsum(
                "hwk,kc->hwc", window, piece[offset_y, offset_x], preferred_element_type=jnp.float32
            )
    return total + bias


def on_device(
    features,
    first_gain,
    first_shift,
    first_weight,
    first_bias,
    second_gain,
    second_shift,
    second_weight,
    second_bias,
    upsample_weight,
    upsample_bias,
):
    height, breadth, channels = features.shape
    normed_one = norm_silu(features.astype(jnp.float32), first_gain, first_shift)
    hidden = convolve(extend(normed_one), first_weight, first_bias, height, breadth).astype(
        jnp.bfloat16
    )
    normed_two = norm_silu(hidden.astype(jnp.float32), second_gain, second_shift)
    block_out = (
        convolve(extend(normed_two), second_weight, second_bias, height, breadth)
        + features.astype(jnp.float32)
    ).astype(jnp.bfloat16)
    doubled = jnp.repeat(jnp.repeat(block_out, 2, axis=0), 2, axis=1)
    padded = extend(doubled)
    return convolve(padded, upsample_weight, upsample_bias, 2 * height, 2 * breadth).astype(
        jnp.bfloat16
    )


def solution(mesh):
    return jax.shard_map(
        on_device,
        mesh=mesh,
        in_specs=(
            P(("img", "row"), "col", None),
            P(),
            P(),
            P(None, None, "row", None),
            P(),
            P(),
            P(),
            P(None, None, "row", None),
            P(),
            P(None, None, "row", None),
            P(),
        ),
        out_specs=P(("img", "row"), "col", None),
        check_vma=False,
    )
```

profile of v0, /device:TPU:1, one launch (start us, length us, event | category | flops | bytes accessed | tf_op | source)
XLA Modules:
  0.0 196.7 jit_solution(13874195632810738690)
XLA Ops:
  8.4 1.7 constant_dynamic-slice_fusion.1
  10.2 1.7 constant_dynamic-slice_fusion
  13.2 31.1 %all-reduce.1 = (f32[32]{0:T(128)S(1)}, f32[32]{0:T(128)S(1)}) all-reduce(f32[32]{0:T(128)S(1)} %reduce_sum.54, f32[32]{0:T(128)S(1)} %reduce_sum.51), channel_id=1, replica_groups=mesh['img'=2,'row'=8,'col'=2] {'row','col'}, use_global_device_ids=true, to_apply=%region_5.6 | all-reduce | flops 64 | bytes 512 | tf_op jit(solution)/shard_map/psum | solution.py:34
  45.6 1.3 collective-permute-start
  46.9 1.3 collective-permute-start.1
  48.2 1.8 collective-permute-done
  50.0 3.9 %collective-permute-done.1 = bf16[1,64,512]{2,1,0:T(8,128)(2,1)S(1)} collective-permute-done((bf16[1,64,512]{2,1,0:T(8,128)(2,1)S(1)}, bf16[1,64,512]{2,1,0:T(8,128)(2,1)S(1)}, u32[]{:S(2)}, u32[]{:S(2)}) %collective-permute-start.1) | collective-permute-done | bytes 65568 | tf_op jit(solution)/shard_map/ppermute | solution.py:22
  53.9 1.3 collective-permute-start.2
  55.2 5.6 %collective-permute-start.3 = (bf16[3,1,512]{2,1,0:T(2,128)(2,1)S(1)}, bf16[3,1,512]{2,1,0:T(2,128)(2,1)S(1)}, u32[]{:S(2)}, u32[]{:S(2)}) collective-permute-start(bf16[3,1,512]{2,1,0:T(2,128)(2,1)S(1)} %get-tuple-element.20), channel_id=1, source_target_pairs={{1,0},{3,2},{5,4},{7,6},{9,8},{11,10},{13,12},{15,14},{17,16},{19,... | collective-permute-start | bytes 9224 | tf_op jit(solution)/shard_map/ppermute | solution.py:22
  60.7 7.4 %all-gather.4.cloned.1.call-done = bf16[3,3,512,512]{3,2,1,0:T(8,128)(2,1)} async-done(((bf16[3,3,32,512]{3,2,1,0:T(8,128)(2,1)}), bf16[3,3,512,512]{3,2,1,0:T(8,128)(2,1)}) %all-gather.4.cloned.1.call-update) | async-done | bytes 4718608 | tf_op jit(solution)/shard_map/all_gather | solution.py:54
  75.6 1.3 fusion.43
  76.9 1.3 fusion.19
  78.2 1.3 fusion.151
  79.9 30.2 %all-reduce = (f32[32]{0:T(128)S(1)}, f32[32]{0:T(128)S(1)}) all-reduce(f32[32]{0:T(128)S(1)} %reduce_sum.75, f32[32]{0:T(128)S(1)} %reduce_sum.72), channel_id=1, replica_groups=mesh['img'=2,'row'=8,'col'=2] {'row','col'}, use_global_device_ids=true, to_apply=%region_11.12 | all-reduce | flops 64 | bytes 512 | tf_op jit(solution)/shard_map/psum | solution.py:34
  110.5 1.3 collective-permute-start.4
  111.8 1.3 collective-permute-start.5
  113.1 10.3 %all-gather.6.cloned.1.call-done = bf16[3,3,512,512]{3,2,1,0:T(8,128)(2,1)} async-done(((bf16[3,3,32,512]{3,2,1,0:T(8,128)(2,1)}), bf16[3,3,512,512]{3,2,1,0:T(8,128)(2,1)}) %all-gather.6.cloned.1.call-update) | async-done | bytes 4718608 | tf_op jit(solution)/shard_map/all_gather | solution.py:54
  124.7 2.2 %collective-permute-start.7 = (bf16[3,1,512]{2,1,0:T(2,128)(2,1)S(1)}, bf16[3,1,512]{2,1,0:T(2,128)(2,1)S(1)}, u32[]{:S(2)}, u32[]{:S(2)}) collective-permute-start(bf16[3,1,512]{2,1,0:T(2,128)(2,1)S(1)} %get-tuple-element.18), channel_id=1, source_target_pairs={{1,0},{3,2},{5,4},{7,6},{9,8},{11,10},{13,12},{15,14},{17,16},{19,... | collective-permute-start | bytes 9224 | tf_op jit(solution)/shard_map/ppermute | solution.py:22
  126.9 1.3 collective-permute-start.6
  130.7 1.3 fusion.39
  132.0 1.3 fusion.37
  134.5 1.2 fusion.35
  135.8 1.3 fusion.13
  137.1 1.3 fusion.27
  138.5 2.4 %collective-permute-start.8 = (bf16[1,128,512]{2,1,0:T(8,128)(2,1)S(1)}, bf16[1,128,512]{2,1,0:T(8,128)(2,1)S(1)}, u32[]{:S(2)}, u32[]{:S(2)}) collective-permute-start(bf16[1,128,512]{2,1,0:T(8,128)(2,1)S(1)} %slice.150), channel_id=1, source_target_pairs={{0,2},{2,4},{4,6},{6,8},{8,10},{10,12},{12,14},{1,3},{3,5},{5,7},{... | collective-permute-start | bytes 393224 | tf_op jit(solution)/shard_map/ppermute | solution.py:20
  140.9 1.3 collective-permute-start.9
  142.2 36.5 %all-gather.8.cloned.1.call-done = bf16[3,3,512,512]{3,2,1,0:T(8,128)(2,1)} async-done(((bf16[3,3,32,512]{3,2,1,0:T(8,128)(2,1)}), bf16[3,3,512,512]{3,2,1,0:T(8,128)(2,1)}) %all-gather.8.cloned.1.call-update) | async-done | bytes 4718608 | tf_op jit(solution)/shard_map/all_gather | solution.py:54
  178.8 1.5 fusion.31
  180.3 1.3 collective-permute-start.10
  181.6 3.0 %collective-permute-start.11 = (bf16[4,1,512]{2,1,0:T(2,128)(2,1)S(1)}, bf16[4,1,512]{2,1,0:T(2,128)(2,1)S(1)}, u32[]{:S(2)}, u32[]{:S(2)}) collective-permute-start(bf16[4,1,512]{2,1,0:T(2,128)(2,1)S(1)} %get-tuple-element.16), channel_id=1, source_target_pairs={{1,0},{3,2},{5,4},{7,6},{9,8},{11,10},{13,12},{15,14},{17,16},{19,... | collective-permute-start | bytes 12296 | tf_op jit(solution)/shard_map/ppermute | solution.py:22
  184.7 1.3 fusion.34
  186.0 1.3 fusion.29
  (78 shorter events, 20.7 us)
Async XLA Ops:
  6.5 1.1 copy-start
  6.5 61.6 %all-gather.4.cloned.1.call-start = ((), (), s32[]{:S(2)}) async-start(), calls=%async_computation | async-start | bytes 5013504 | tf_op jit(solution)/shard_map/all_gather | solution.py:54
  8.4 69.8 %copy-start.3 = (f32[512]{0:T(512)S(1)}, f32[512]{0:T(512)}, u32[]{:S(2)}) copy-start(f32[512]{0:T(512)} %param.15) | copy-start | bytes 6148
  8.4 115.0 %all-gather.6.cloned.1.call-start = ((), (), s32[]{:S(2)}) async-start(), calls=%async_computation.1 | async-start | bytes 5013504 | tf_op jit(solution)/shard_map/all_gather | solution.py:54
  10.2 168.6 %all-gather.8.cloned.1.call-start = ((), (), s32[]{:S(2)}) async-start(), calls=%async_computation.2 | async-start | bytes 5013504 | tf_op jit(solution)/shard_map/all_gather | solution.py:54
  11.9 98.5 %copy-start.4 = (f32[512]{0:T(512)S(1)}, f32[512]{0:T(512)}, u32[]{:S(2)}) copy-start(f32[512]{0:T(512)} %param.17) | copy-start | bytes 6148
  11.9 98.5 %copy-start.5 = (f32[512]{0:T(512)S(1)}, f32[512]{0:T(512)}, u32[]{:S(2)}) copy-start(f32[512]{0:T(512)} %param.16) | copy-start | bytes 6148
  45.6 4.4 %collective-permute-start = (bf16[1,64,512]{2,1,0:T(8,128)(2,1)S(1)}, bf16[1,64,512]{2,1,0:T(8,128)(2,1)S(1)}, u32[]{:S(2)}, u32[]{:S(2)}) collective-permute-start(bf16[1,64,512]{2,1,0:T(8,128)(2,1)S(1)} %fusion.69), channel_id=1, source_target_pairs={{0,2},{2,4},{4,6},{6,8},{8,10},{10,12},{12,14},{1,3},{3,5},{5,7},{... | collective-permute-start | bytes 196616 | tf_op jit(solution)/shard_map/ppermute | solution.py:20
  46.9 6.9 %collective-permute-start.1 = (bf16[1,64,512]{2,1,0:T(8,128)(2,1)S(1)}, bf16[1,64,512]{2,1,0:T(8,128)(2,1)S(1)}, u32[]{:S(2)}, u32[]{:S(2)}) collective-permute-start(bf16[1,64,512]{2,1,0:T(8,128)(2,1)S(1)} %fusion.69), channel_id=1, source_target_pairs={{2,0},{4,2},{6,4},{8,6},{10,8},{12,10},{14,12},{3,1},{5,3},{7,5},{... | collective-permute-start | bytes 196616 | tf_op jit(solution)/shard_map/ppermute | solution.py:22
  53.9 6.9 %collective-permute-start.2 = (bf16[3,1,512]{2,1,0:T(2,128)(2,1)S(1)}, bf16[3,1,512]{2,1,0:T(2,128)(2,1)S(1)}, u32[]{:S(2)}, u32[]{:S(2)}) collective-permute-start(bf16[3,1,512]{2,1,0:T(2,128)(2,1)S(1)} %get-tuple-element.19), channel_id=1, source_target_pairs={{0,1},{2,3},{4,5},{6,7},{8,9},{10,11},{12,13},{14,15},{16,17},{18,... | collective-permute-start | bytes 9224 | tf_op jit(solution)/shard_map/ppermute | solution.py:20
  55.2 15.4 %collective-permute-start.3 = (bf16[3,1,512]{2,1,0:T(2,128)(2,1)S(1)}, bf16[3,1,512]{2,1,0:T(2,128)(2,1)S(1)}, u32[]{:S(2)}, u32[]{:S(2)}) collective-permute-start(bf16[3,1,512]{2,1,0:T(2,128)(2,1)S(1)} %get-tuple-element.20), channel_id=1, source_target_pairs={{1,0},{3,2},{5,4},{7,6},{9,8},{11,10},{13,12},{15,14},{17,16},{19,... | collective-permute-start | bytes 9224 | tf_op jit(solution)/shard_map/ppermute | solution.py:22
  78.2 58.8 %copy-start.2 = (bf16[1,64,512]{2,1,0:T(8,128)(2,1)S(1)}, bf16[1,64,512]{2,1,0:T(8,128)(2,1)}, u32[]{:S(2)}) copy-start(bf16[1,64,512]{2,1,0:T(8,128)(2,1)} %param.11) | copy-start | bytes 196612
  78.2 58.8 %copy-start.6 = (f32[512]{0:T(512)S(1)}, f32[512]{0:T(512)}, u32[]{:S(2)}) copy-start(f32[512]{0:T(512)} %param.19) | copy-start | bytes 6148
  110.5 14.2 %collective-permute-start.4 = (bf16[1,64,512]{2,1,0:T(8,128)(2,1)S(1)}, bf16[1,64,512]{2,1,0:T(8,128)(2,1)S(1)}, u32[]{:S(2)}, u32[]{:S(2)}) collective-permute-start(bf16[1,64,512]{2,1,0:T(8,128)(2,1)S(1)} %fusion.153), channel_id=1, source_target_pairs={{0,2},{2,4},{4,6},{6,8},{8,10},{10,12},{12,14},{1,3},{3,5},{5,7},{... | collective-permute-start | bytes 196616 | tf_op jit(solution)/shard_map/ppermute | solution.py:20
  111.8 12.9 %collective-permute-start.5 = (bf16[1,64,512]{2,1,0:T(8,128)(2,1)S(1)}, bf16[1,64,512]{2,1,0:T(8,128)(2,1)S(1)}, u32[]{:S(2)}, u32[]{:S(2)}) collective-permute-start(bf16[1,64,512]{2,1,0:T(8,128)(2,1)S(1)} %fusion.153), channel_id=1, source_target_pairs={{2,0},{4,2},{6,4},{8,6},{10,8},{12,10},{14,12},{3,1},{5,3},{7,5},{... | collective-permute-start | bytes 196616 | tf_op jit(solution)/shard_map/ppermute | solution.py:22
  124.7 8.5 %collective-permute-start.7 = (bf16[3,1,512]{2,1,0:T(2,128)(2,1)S(1)}, bf16[3,1,512]{2,1,0:T(2,128)(2,1)S(1)}, u32[]{:S(2)}, u32[]{:S(2)}) collective-permute-start(bf16[3,1,512]{2,1,0:T(2,128)(2,1)S(1)} %get-tuple-element.18), channel_id=1, source_target_pairs={{1,0},{3,2},{5,4},{7,6},{9,8},{11,10},{13,12},{15,14},{17,16},{19,... | collective-permute-start | bytes 9224 | tf_op jit(solution)/shard_map/ppermute | solution.py:22
  126.9 3.8 %collective-permute-start.6 = (bf16[3,1,512]{2,1,0:T(2,128)(2,1)S(1)}, bf16[3,1,512]{2,1,0:T(2,128)(2,1)S(1)}, u32[]{:S(2)}, u32[]{:S(2)}) collective-permute-start(bf16[3,1,512]{2,1,0:T(2,128)(2,1)S(1)} %get-tuple-element.17), channel_id=1, source_target_pairs={{0,1},{2,3},{4,5},{6,7},{8,9},{10,11},{12,13},{14,15},{16,17},{18,... | collective-permute-start | bytes 9224 | tf_op jit(solution)/shard_map/ppermute | solution.py:20
  138.5 41.7 %collective-permute-start.8 = (bf16[1,128,512]{2,1,0:T(8,128)(2,1)S(1)}, bf16[1,128,512]{2,1,0:T(8,128)(2,1)S(1)}, u32[]{:S(2)}, u32[]{:S(2)}) collective-permute-start(bf16[1,128,512]{2,1,0:T(8,128)(2,1)S(1)} %slice.150), channel_id=1, source_target_pairs={{0,2},{2,4},{4,6},{6,8},{8,10},{10,12},{12,14},{1,3},{3,5},{5,7},{... | collective-permute-start | bytes 393224 | tf_op jit(solution)/shard_map/ppermute | solution.py:20
  140.9 39.3 %collective-permute-start.9 = (bf16[1,128,512]{2,1,0:T(8,128)(2,1)S(1)}, bf16[1,128,512]{2,1,0:T(8,128)(2,1)S(1)}, u32[]{:S(2)}, u32[]{:S(2)}) collective-permute-start(bf16[1,128,512]{2,1,0:T(8,128)(2,1)S(1)} %slice.150), channel_id=1, source_target_pairs={{2,0},{4,2},{6,4},{8,6},{10,8},{12,10},{14,12},{3,1},{5,3},{7,5},{... | collective-permute-start | bytes 393224 | tf_op jit(solution)/shard_map/ppermute | solution.py:22
  178.8 8.8 %copy-start.1 = (bf16[3,3,512,512]{3,2,1,0:T(8,128)(2,1)S(1)}, bf16[3,3,512,512]{3,2,1,0:T(8,128)(2,1)}, u32[]{:S(2)}) copy-start(bf16[3,3,512,512]{3,2,1,0:T(8,128)(2,1)} %all-gather.8.cloned.1.call-done) | copy-start | bytes 14155780
  180.3 7.0 %collective-permute-start.10 = (bf16[4,1,512]{2,1,0:T(2,128)(2,1)S(1)}, bf16[4,1,512]{2,1,0:T(2,128)(2,1)S(1)}, u32[]{:S(2)}, u32[]{:S(2)}) collective-permute-start(bf16[4,1,512]{2,1,0:T(2,128)(2,1)S(1)} %get-tuple-element.15), channel_id=1, source_target_pairs={{0,1},{2,3},{4,5},{6,7},{8,9},{10,11},{12,13},{14,15},{16,17},{18,... | collective-permute-start | bytes 12296 | tf_op jit(solution)/shard_map/ppermute | solution.py:20
  181.6 5.7 %collective-permute-start.11 = (bf16[4,1,512]{2,1,0:T(2,128)(2,1)S(1)}, bf16[4,1,512]{2,1,0:T(2,128)(2,1)S(1)}, u32[]{:S(2)}, u32[]{:S(2)}) collective-permute-start(bf16[4,1,512]{2,1,0:T(2,128)(2,1)S(1)} %get-tuple-element.16), channel_id=1, source_target_pairs={{1,0},{3,2},{5,4},{7,6},{9,8},{11,10},{13,12},{15,14},{17,16},{19,... | collective-permute-start | bytes 12296 | tf_op jit(solution)/shard_map/ppermute | solution.py:22
  187.5 1.6 copy-start.7
Sparse Core Ops, SparseCore 0:
  9.5 58.5 all-gather.3
  70.3 53.0 all-gather.5
  125.6 53.0 all-gather.7
where the time goes:
time: 198 us; the launch traced here: 197 us
  blocking collectives  61.3 us (31%)
  waiting for transfers between devices  59.9 us (30%)
  matrix products  29.3 us (15%)
  starting transfers between devices  23.6 us (12%)
  between operations  13.6 us (7%)
  local copies, waits for them, and re-layouts  6.39 us (3%)
  other arithmetic  2.58 us (1%)
    psum x2, blocking collectives, norm_silu(): total, squares = lax.psum((total, squares), ('row', 'col'))  61.3 us
    all_gather x3, waiting for transfers between devices, convolve(): piece = lax.all_gather(own, ('row', 'col'), axis=2, tiled=True)  54.2 us
    dot_general x27, matrix products, convolve(): jnp.einsum('hwk,kc->hwc', window, piece[offset_y, offset_x], preferred_el...  29.3 us
    ppermute x6, starting transfers between devices, extended(): lax.ppermute(head, axis, [((i + 1) % count, i) for i in range(ends)])  14.6 us
    ppermute x6, starting transfers between devices, extended(): lax.ppermute(tail, axis, [(i, (i + 1) % count) for i in range(ends)])  8.86 us
    dynamic_slice x3, local copies, waits for them, and re-layouts, convolve(): lax.dynamic_slice_in_dim(weight, lax.axis_index('col') * share, share, 2)  4.17 us
  transfers between devices with their start and end apart: 15, of which 5 were waited for; matrix products, arithmetic and copies ran while one was open for 17% of the time, Pallas kernels for 0%

commit v1 on v0

--- a/solution.py
+++ b/solution.py
@@ -1,6 +1,8 @@
 import jax
 import jax.numpy as jnp
 from jax import lax
+from jax.experimental import pallas as pl
+from jax.experimental.pallas import tpu as pltpu
 from jax.sharding import PartitionSpec as P
 
 G = 32
@@ -95,9 +97,636 @@
     )
 
 
+def fused_kernel(
+    features,
+    gain_one,
+    shift_one,
+    bias_one,
+    gain_two,
+    shift_two,
+    bias_two,
+    bias_up,
+    weight_one,
+    weight_two,
+    weight_up,
+    out,
+    fbuf,
+    xs,
+    taps,
+    gathered,
+    parts,
+    sums,
+    hbuf,
+    stats,
+    own_block,
+    b3,
+    x3,
+    mixed,
+    swap,
+    local_sem,
+    wx_send,
+    wx_recv,
+    f_send,
+    f_recv,
+    rs_send,
+    rs_recv,
+    h_send,
+    h_recv,
+    b_send,
+    b_recv,
+    ring_send,
+    ring_recv,
+    y_send,
+    y_recv,
+    o_send,
+    o_recv,
+):
+    img = lax.axis_index("img")
+    row = lax.axis_index("row")
+    col = lax.axis_index("col")
+    rows = lax.axis_size("row")
+    cuts = rows // 2
+    z, x = row // 2, row % 2
+    other = 1 - col
+    pair = row + 1 - 2 * x
+    half_width, channels = features.shape
+    width = 2 * half_width
+    block = channels // cuts
+    share = channels // rows
+    outs = channels // 2
+    near = rows // 2
+    f32, bf16 = jnp.float32, jnp.bfloat16
+    pending = []
+
+    def remote(src, dst, send, recv, **device):
+        return pltpu.make_async_remote_copy(
+            src_ref=src,
+            dst_ref=dst,
+            send_sem=send,
+            recv_sem=recv,
+            device_id=device,
+            device_id_type=pl.DeviceIdType.MESH,
+        )
+
+    zero_rows = jnp.zeros((2, width, block), bf16)
+    for parity in range(2):
+        for slot in (0, 2):
+            b3[parity, slot] = zero_rows
+
+    barrier = pltpu.get_barrier_semaphore()
+    for step in range(rows):
+        for side in range(2):
+            if step or side:
+                pl.semaphore_signal(
+                    barrier,
+                    inc=1,
+                    device_id={"row": (row + step) % rows, "col": (col + side) % 2},
+                    device_id_type=pl.DeviceIdType.MESH,
+                )
+    pl.semaphore_signal(
+        barrier, inc=1, device_id={"img": 1 - img}, device_id_type=pl.DeviceIdType.MESH
+    )
+    pl.semaphore_wait(barrier, 2 * rows)
+
+    lanes = pl.ds(pl.multiple_of(col * outs, outs), outs)
+    mine = pl.ds(pl.multiple_of(x * share, share), share)
+
+    def feature_copy(step):
+        target = (row + step) % rows
+        part = pl.ds(pl.multiple_of((target // 2) * block, block), block)
+        return remote(
+            features.at[:, part], fbuf.at[col, row], f_send.at[step], f_recv.at[row], row=target
+        )
+
+    for step in range(1, rows):
+        copy = feature_copy(step)
+        copy.start()
+        pending.append(copy)
+    fbuf[col, row] = features[:, pl.ds(pl.multiple_of(z * block, block), block)]
+
+    local = []
+    for index, weight in enumerate((weight_one, weight_two)):
+        copy = remote(
+            weight.at[:, :, :, lanes],
+            taps.at[index, :, :, mine, :],
+            wx_send.at[index],
+            wx_recv.at[index],
+            row=pair,
+        )
+        copy.start()
+        pending.append(copy)
+        copy = pltpu.make_async_copy(
+            weight.at[:, :, :, lanes], taps.at[index, :, :, mine, :], local_sem.at[index]
+        )
+        copy.start()
+        local.append(copy)
+    copy = pltpu.make_async_copy(
+        weight_up.at[:, :, :, lanes],
+        gathered.at[:, :, pl.ds(pl.multiple_of(row * share, share), share), :],
+        local_sem.at[2],
+    )
+    copy.start()
+    local.append(copy)
+
+    place = z * (1 - x) + (rows - 1 - z) * x
+    piece = share // 2
+
+    def row_at(position):
+        side = position // near
+        return (1 - side) * 2 * position + side * (2 * (rows - 1 - position) + 1)
+
+    after = row_at((place + 1) % rows)
+    before = row_at((place + rows - 1) % rows)
+
+    def unit(position, part):
+        return gathered.at[
+            :, :, pl.ds(pl.multiple_of(row_at(position) * share + part * piece, piece), piece), :
+        ]
+
+    def ring_copy(way, step):
+        position = (place + rows - (step - 1)) % rows if way == 0 else (place + step - 1) % rows
+        if step == 1:
+            src = weight_up.at[:, :, pl.ds(pl.multiple_of(img * piece, piece), piece), lanes]
+        else:
+            src = unit(position, img)
+        return remote(
+            src,
+            unit(position, img),
+            ring_send.at[way, step - 1],
+            ring_recv.at[way, step - 1],
+            row=after if way == 0 else before,
+        )
+
+    reach = (near, rows - 1 - near)
+
+    def cross_copy(way, step, half):
+        position = (place + rows - step) % rows if way == 0 else (place + step) % rows
+        return remote(
+            unit(position, half),
+            unit(position, half),
+            y_send.at[way, step - 1],
+            y_recv.at[way, step - 1],
+            img=1 - img,
+        )
+
+    def start_ring(step):
+        for way in range(2):
+            if step <= reach[way]:
+                copy = ring_copy(way, step)
+                copy.start()
+                pending.append(copy)
+
+    def arrived_ring(way, step):
+        position = (place + rows - step) % rows if way == 0 else (place + step) % rows
+        return remote(
+            unit(position, img),
+            unit(position, img),
+            ring_send.at[way, step - 1],
+            ring_recv.at[way, step - 1],
+            row=after,
+        )
+
+    def turn_ring(step):
+        for way in range(2):
+            if step <= reach[way]:
+                arrived_ring(way, step).wait_recv()
+        start_ring(step + 1)
+        for way in range(2):
+            if step <= reach[way]:
+                copy = cross_copy(way, step, img)
+                copy.start()
+                pending.append(copy)
+
+    start_ring(1)
+
+    for step in range(1, rows):
+        origin = (row + step) % rows
+        remote(
+            features.at[:, pl.ds(0, block)],
+            fbuf.at[col, origin],
+            f_send.at[step],
+            f_recv.at[origin],
+            row=pair,
+        ).wait_recv()
+    copy = remote(fbuf.at[col], fbuf.at[col], f_send.at[0], f_recv.at[rows], col=other)
+    copy.start()
+    pending.append(copy)
+    remote(fbuf.at[other], fbuf.at[other], f_send.at[0], f_recv.at[rows], col=other).wait_recv()
+
+    same = (
+        lax.broadcasted_iota(jnp.int32, (block, block), 0) // (channels // G)
+        == lax.broadcasted_iota(jnp.int32, (block, block), 1) // (channels // G)
+    ).astype(f32)
+    count = rows * width * (channels // G)
+
+    def moments(total, squares):
+        both = jnp.concatenate([total, squares, jnp.zeros((6, block), f32)], axis=0)
+        both = jnp.dot(both, same, precision=lax.Precision.HIGHEST, preferred_element_type=f32)
+        mean = both[0:1] / count
+        var = both[1:2] / count - mean * mean
+        return mean, lax.rsqrt(var + EPS)
+
+    here = pl.ds(pl.multiple_of(z * block, block), block)
+    first_column = lax.broadcasted_iota(jnp.int32, (width, block), 0) == 0
+    last_column = lax.broadcasted_iota(jnp.int32, (width, block), 0) == width - 1
+
+    def fill(slot, values, mean, factor, gain, shift):
+        normed = (values - mean) * factor * gain + shift
+        normed = normed / (1.0 + jnp.exp(-normed))
+        if slot == 0:
+            normed = jnp.where(x == 0, 0.0, normed)
+        if slot == near + 1:
+            normed = jnp.where(x == 1, 0.0, normed)
+        left = jnp.where(first_column, 0.0, pltpu.roll(normed, 1, 0))
+        right = jnp.where(last_column, 0.0, pltpu.roll(normed, width - 1, 0))
+        xs[slot, :, 0:block] = left.astype(bf16)
+        xs[slot, :, block : 2 * block] = normed.astype(bf16)
+        xs[slot, :, 2 * block : 3 * block] = right.astype(bf16)
+
+    def feature_row(index):
+        return jnp.concatenate([fbuf[0, index], fbuf[1, index]], axis=0).astype(f32)
+
+    total = jnp.zeros((1, block), f32)
+    squares = jnp.zeros((1, block), f32)
+    for index in range(rows):
+        values = feature_row(index)
+        total += jnp.sum(values, axis=0, keepdims=True)
+        squares += jnp.sum(values * values, axis=0, keepdims=True)
+    mean, factor = moments(total, squares)
+    for slot in range(near + 2):
+        index = jnp.clip(near * x - 1 + slot, 0, rows - 1)
+        fill(slot, feature_row(index), mean, factor, gain_one[:, here], shift_one[:, here])
+
+    tile = near * width // 2
+
+    def partial_conv(index):
+        local[index].wait()
+        remote(
+            weight_one.at[:, :, :, lanes],
+            taps.at[index, :, :, pl.ds(pl.multiple_of((1 - x) * share, share), share), :],
+            wx_send.at[index],
+            wx_recv.at[index],
+            row=pair,
+        ).wait_recv()
+        for side in range(2):
+            acc = jnp.zeros((tile, outs), f32)
+            for a in range(3):
+                first = a + side * near // 2
+                acc += jnp.dot(
+                    xs[first : first + near // 2].reshape(tile, 3 * block),
+                    taps[index, a].reshape(3 * block, outs),
+                    preferred_element_type=f32,
+                )
+            for j in range(2):
+                parts[index, j, side] = acc[:, j * block : (j + 1) * block].astype(bf16)
+                target = 2 * col + j
+                itself = jnp.logical_and(target == z, col == side)
+                copy = remote(
+                    parts.at[index, j, side],
+                    sums.at[index, z],
+                    rs_send.at[index, j, side],
+                    rs_recv.at[index, z],
+                    row=2 * target + x,
+                    col=side,
+                )
+
+                @pl.when(itself)
+                def _():
+                    sums[index, z] = parts[index, j, side]
+
+                @pl.when(jnp.logical_not(itself))
+                def _():
+                    copy.start()
+
+    def partial_sent(index):
+        for side in range(2):
+            for j in range(2):
+                target = 2 * col + j
+
+                @pl.when(jnp.logical_not(jnp.logical_and(target == z, col == side)))
+                def _():
+                    remote(
+                        parts.at[index, j, side],
+                        sums.at[index, z],
+                        rs_send.at[index, j, side],
+                        rs_recv.at[index, z],
+                        row=2 * target + x,
+                        col=side,
+                    ).wait_send()
+
+    def reduced(index, bias):
+        for origin in range(cuts):
+
+            @pl.when(jnp.logical_not(jnp.logical_and(z == origin, z // 2 == col)))
+            def _():
+                remote(
+                    parts.at[index, 0, 0],
+                    sums.at[index, origin],
+                    rs_send.at[index, 0, 0],
+                    rs_recv.at[index, origin],
+                    row=pair,
+                ).wait_recv()
+
+        result = sums[index, 0].astype(f32)
+        for origin in range(1, cuts):
+            result += sums[index, origin].astype(f32)
+        return result + bias[:, here]
+
+    partial_conv(0)
+    turn_ring(1)
+
+    hidden = reduced(0, bias_one).astype(bf16)
+    start = 1 + 2 * col
+    hbuf[pl.ds(start, 2)] = hidden.reshape(2, width, block)
+    hidden = hidden.astype(f32)
+    group = 2 * x + col
+    stats[group] = jnp.concatenate(
+        [
+            jnp.sum(hidden, axis=0, keepdims=True),
+            jnp.sum(hidden * hidden, axis=0, keepdims=True),
+            jnp.zeros((6, block), f32),
+        ],
+        axis=0,
+    )
+    for step, (target_row, target_col) in enumerate(((row, other), (pair, col), (pair, other))):
+        copy = remote(
+            stats.at[group],
+            stats.at[group],
+            h_send.at[step],
+            h_recv.at[group],
+            row=target_row,
+            col=target_col,
+        )
+        copy.start()
+        pending.append(copy)
+    copy = remote(
+        hbuf.at[pl.ds(start, 2)], hbuf.at[pl.ds(start, 2)], h_send.at[3], h_recv.at[4], col=other
+    )
+    copy.start()
+    pending.append(copy)
+
+    def edge(side):
+        return remote(
+            hbuf.at[near - (near - 1) * x],
+            hbuf.at[(near + 1) * x],
+            h_send.at[4 + side],
+            h_recv.at[5],
+            row=pair,
+            col=side,
+        )
+
+    @pl.when(col == 1 - x)
+    def _():
+        for side in range(2):
+            edge(side).start()
+
+    turn_ring(2)
+    for who in range(4):
+
+        @pl.when(group != who)
+        def _():
+            remote(
+                stats.at[who], stats.at[who], h_send.at[0], h_recv.at[who], row=pair
+            ).wait_recv()
+
+    theirs = hbuf.at[pl.ds(1 + 2 * other, 2)]
+    remote(theirs, theirs, h_send.at[3], h_recv.at[4], col=other).wait_recv()
+    remote(
+        hbuf.at[0], hbuf.at[(near + 1) * (1 - x)], h_send.at[4], h_recv.at[5], row=pair
+    ).wait_recv()
+    both = stats[0] + stats[1] + stats[2] + stats[3]
+    mean, factor = moments(both[0:1], both[1:2])
+    for slot in range(near + 2):
+        values = hbuf[slot].astype(f32)
+        if slot == 0:
+            values = jnp.where(x == 0, 0.0, values)
+        if slot == near + 1:
+            values = jnp.where(x == 1, 0.0, values)
+        fill(slot, values, mean, factor, gain_two[:, here], shift_two[:, here])
+
+    partial_conv(1)
+    turn_ring(3)
+
+    residual = jnp.concatenate(
+        [feature_row(near * x + 2 * col), feature_row(near * x + 2 * col + 1)], axis=0
+    )
+    own_block[...] = (reduced(1, bias_two) + residual).astype(bf16).reshape(2, width, block)
+
+    def block_copies(act):
+        for k in range(2):
+            origin = near * x + 2 * col + k
+            for d in (-1, 0, 1):
+                target = origin + d
+                valid = jnp.logical_and(target >= 0, target < rows)
+                itself = jnp.logical_and(target == row, z % 2 == col)
+                act(k, d, target, valid, itself)
+
+    def block_copy(k, d, target):
+        return remote(
+            own_block.at[k],
+            b3.at[z % 2, 1 - d, z // 2],
+            b_send.at[k, d + 1],
+            b_recv.at[1 - d, z // 2],
+            row=target,
+            col=z % 2,
+        )
+
+    def begin(k, d, target, valid, itself):
+        @pl.when(jnp.logical_and(valid, jnp.logical_not(itself)))
+        def _():
+            block_copy(k, d, target).start()
+
+        @pl.when(itself)
+        def _():
+            b3[z % 2, 1 - d, z // 2] = own_block[k]
+
+    def finish(k, d, target, valid, itself):
+        @pl.when(jnp.logical_and(valid, jnp.logical_not(itself)))
+        def _():
+            block_copy(k, d, target).wait_send()
+
+    block_copies(begin)
+    turn_ring(4)
+    for slot in range(3):
+        source = row + slot - 1
+        valid = jnp.logical_and(source >= 0, source < rows)
+        for half in range(2):
+            block_of = 2 * half + col
+            itself = jnp.logical_and(
+                jnp.logical_and(block_of == z, source // near == x), (source // 2) % 2 == col
+            )
+
+            @pl.when(jnp.logical_and(valid, jnp.logical_not(itself)))
+            def _():
+                remote(
+                    own_block.at[0],
+                    b3.at[col, slot, half],
+                    b_send.at[0, 0],
+                    b_recv.at[slot, half],
+                    row=pair,
+                ).wait_recv()
+
+    copy = remote(b3.at[col], b3.at[col], b_send.at[2, 0], b_recv.at[3, 0], col=other)
+    copy.start()
+    pending.append(copy)
+    remote(b3.at[other], b3.at[other], b_send.at[2, 0], b_recv.at[3, 0], col=other).wait_recv()
+
+    for slot in range(3):
+        for which in range(cuts):
+            at = slice(which * block, (which + 1) * block)
+            values = b3[which % 2, slot, which // 2]
+            wide = values.astype(f32)
+            x3[slot, 0, :, at] = jnp.where(first_column, 0.0, pltpu.roll(wide, 1, 0)).astype(bf16)
+            x3[slot, 1, :, at] = values
+            x3[slot, 2, :, at] = jnp.where(
+                last_column, 0.0, pltpu.roll(wide, width - 1, 0)
+            ).astype(bf16)
+
+    local[2].wait()
+    for way in range(2):
+        for step in range(1, reach[way] + 1):
+            cross_copy(way, step, 1 - img).wait_recv()
+
+    acc = jnp.zeros((4 * width, outs), f32)
+    for a in range(3):
+        for c in range(3):
+            window = jnp.concatenate(
+                [
+                    x3[(p + a - 1) // 2 + 1, (q + c - 1) // 2 + 1]
+                    for p in range(2)
+                    for q in range(2)
+                ],
+                axis=0,
+            )
+            acc += jnp.dot(window, gathered[a, c], preferred_element_type=f32)
+    acc += bias_up[:, lanes]
+    for p in range(2):
+        for q in range(2):
+            first = (2 * p + q) * width
+            for lane in range(outs // 128):
+                mixed[lane, p, pl.ds(q, width, stride=2), :] = acc[
+                    first : first + width, lane * 128 : (lane + 1) * 128
+                ]
+    for p in range(2):
+        for lane in range(outs // 128):
+            at = slice(lane * 128, (lane + 1) * 128)
+            swap[p, :, at] = mixed[
+                lane, p, pl.ds(pl.multiple_of(other * width, width), width), :
+            ].astype(bf16)
+    copy = remote(swap, out.at[:, :, lanes], o_send.at[0], o_recv.at[0], col=other)
+    copy.start()
+    pending.append(copy)
+    for p in range(2):
+        for lane in range(outs // 128):
+            at = pl.ds(pl.multiple_of(col * outs + lane * 128, 128), 128)
+            out[p, :, at] = mixed[
+                lane, p, pl.ds(pl.multiple_of(col * width, width), width), :
+            ].astype(bf16)
+    their_lanes = pl.ds(pl.multiple_of(other * outs, outs), outs)
+    remote(swap, out.at[:, :, their_lanes], o_send.at[0], o_recv.at[0], col=other).wait_recv()
+
+    for copy in pending:
+        copy.wait_send()
+    partial_sent(0)
+    partial_sent(1)
+    block_copies(finish)
+
+    @pl.when(col == 1 - x)
+    def _():
+        for side in range(2):
+            edge(side).wait_send()
+
+
+def fused(
+    features,
+    first_gain,
+    first_shift,
+    first_weight,
+    first_bias,
+    second_gain,
+    second_shift,
+    second_weight,
+    second_bias,
+    upsample_weight,
+    upsample_bias,
+):
+    _, half_width, channels = features.shape
+    rows = lax.axis_size("row")
+    cuts, near, width = rows // 2, rows // 2, 2 * half_width
+    block, outs = channels // cuts, channels // 2
+    bf16, f32 = jnp.bfloat16, jnp.float32
+    dma = pltpu.SemaphoreType.DMA
+    vmem = pl.BlockSpec(memory_space=pltpu.VMEM)
+    anywhere = pl.BlockSpec(memory_space=pl.ANY)
+    vectors = [
+        v.reshape(1, channels)
+        for v in (
+            first_gain,
+            first_shift,
+            first_bias,
+            second_gain,
+            second_shift,
+            second_bias,
+            upsample_bias,
+        )
+    ]
+    return pl.pallas_call(
+        fused_kernel,
+        out_shape=jax.ShapeDtypeStruct((2, width, channels), bf16),
+        in_specs=[vmem] * 8 + [anywhere] * 3,
+        out_specs=vmem,
+        scratch_shapes=[
+            pltpu.VMEM((2, rows, half_width, block), bf16),
+            pltpu.VMEM((near + 2, width, 3 * block), bf16),
+            pltpu.VMEM((2, 3, 3, block, outs), bf16),
+            pltpu.VMEM((3, 3, channels, outs), bf16),
+            pltpu.VMEM((2, 2, 2, near * width // 2, block), bf16),
+            pltpu.VMEM((2, cuts, near * width // 2, block), bf16),
+            pltpu.VMEM((near + 2, width, block), bf16),
+            pltpu.VMEM((4, 8, block), f32),
+            pltpu.VMEM((2, width, block), bf16),
+            pltpu.VMEM((2, 3, 2, width, block), bf16),
+            pltpu.VMEM((3, 3, width, channels), bf16),
+            pltpu.VMEM((outs // 128, 2, 2 * width, 128), f32),
+            pltpu.VMEM((2, width, outs), bf16),
+            dma((3,)),
+            dma((2,)),
+            dma((2,)),
+            dma((rows,)),
+            dma((rows + 1,)),
+            dma((2, 2, 2)),
+            dma((2, cuts)),
+            dma((6,)),
+            dma((6,)),
+            dma((3, 3)),
+            dma((4, 2)),
+            dma((2, near)),
+            dma((2, near)),
+            dma((2, near)),
+            dma((2, near)),
+            dma((1,)),
+            dma((1,)),
+        ],
+        compiler_params=pltpu.CompilerParams(collective_id=0, has_side_effects=True),
+    )(features.reshape(half_width, channels), *vectors, first_weight, second_weight, upsample_weight)
+
+
+def program(features, *others):
+    height, half_width, channels = features.shape
+    rows = lax.axis_size("row")
+    fits = (
+        (lax.axis_size("img"), rows, lax.axis_size("col")) == (2, 8, 2)
+        and height == 1
+        and half_width % 16 == 0
+        and channels == rows // 2 * 128
+        and 128 % (channels // G) == 0
+    )
+    return (fused if fits else on_device)(features, *others)
+
+
 def solution(mesh):
     return jax.shard_map(
-        on_device,
+        program,
         mesh=mesh,
         in_specs=(
             P(("img", "row"), "col", None),

time: 198 us -> 55.9 us (0.28)
  blocking collectives: 61.3 us -> 0 us
  waiting for transfers between devices: 59.9 us -> 0 us
  Pallas kernels: 0 us -> 54 us
  matrix products: 29.3 us -> 0 us
  starting transfers between devices: 23.6 us -> 0 us
  between operations: 13.6 us -> 0.01 us
  local copies, waits for them, and re-layouts: 6.39 us -> 1.67 us
  other arithmetic: 2.58 us -> 0 us
    psum x2 -> x0, blocking collectives: 61.3 us -> none  [norm_silu(): total, squares = lax.psum((total, squares), ('row', 'col'))]
    all_gather x3 -> x0, waiting for transfers between devices: 54.2 us -> none  [convolve(): piece = lax.all_gather(own, ('row', 'col'), axis=2, tiled=True)]
    pallas_call x0 -> x1, Pallas kernels: none -> 54 us  [fused(): pl.pallas_call(fused_kernel, out_shape=jax.ShapeDtypeStruct((2, width, ch...]
    dot_general x27 -> x0, matrix products: 29.3 us -> none  [convolve(): jnp.einsum('hwk,kc->hwc', window, piece[offset_y, offset_x], preferred_el...]
    ppermute x12 -> x0, starting transfers between devices: 23.5 us -> none  [the longest x6 14.6 us: extended(): lax.ppermute(head, axis, [((i + 1) % count, i) for i in range(ends)])]
    ppermute x12 -> x0, waiting for transfers between devices: 5.66 us -> none  [the longest x6 3.89 us: extended(): lax.ppermute(head, axis, [((i + 1) % count, i) for i in range(ends)])]
    dynamic_slice x3 -> x0, local copies, waits for them, and re-layouts: 4.17 us -> none  [convolve(): lax.dynamic_slice_in_dim(weight, lax.axis_index('col') * share, share, 2)]
  transfers between devices with their start and end apart: 15 -> 0, of which waited for: 5 -> 0; matrix products, arithmetic and copies ran while one was open for 17% -> 0% of each run, Pallas kernels for 0% -> 0%
where the time goes in v1:
time: 55.9 us; the launch traced here: 55.7 us
  Pallas kernels  54 us (97%)
  local copies, waits for them, and re-layouts  1.67 us (3%)
    pallas_call x1, Pallas kernels, fused(): pl.pallas_call(fused_kernel, out_shape=jax.ShapeDtypeStruct((2, width, ch...  54 us
    unnamed x1, local copies, waits for them, and re-layouts  1.67 us

profile of v1, /device:TPU:1, one launch (start us, length us, event | category | flops | bytes accessed | tf_op | source)
XLA Modules:
  0.0 55.7 jit_solution(16455104572229333141)
XLA Ops:
  0.0 54.0 %shard_map.109 = bf16[2,128,512]{2,1,0:T(8,128)(2,1)} custom-call(bf16[64,512]{1,0:T(8,128)(2,1)} %bitcast.8, f32[1,512]{1,0:T(1,128)} %bitcast.9, f32[1,512]{1,0:T(1,128)} %bitcast.10, f32[1,512]{1,0:T(1,128)} %bitcast.11, f32[1,512]{1,0:T(1,128)} %bitcast.12, f32[1,512]{1,0:T(1,128)} %bitcast.13, f32[1,512]{1,0:T(1,128)} %bitcast.14, f32[1,512]{1,0:T(1,128)} %bitcast.15, ...), custom_call_target="tpu_custom_call" | custom-call | tf_op jit(solution)/shard_map/pallas_call | solution.py:673
  54.0 1.7 %copy.13 = bf16[2,128,512]{2,1,0:T(8,128)(2,1)} copy(bf16[2,128,512]{2,1,0:T(8,128)(2,1)} %shard_map.109) | data formatting | bytes 524288

commit v2 on v1

--- a/solution.py
+++ b/solution.py
@@ -204,10 +204,9 @@
         pending.append(copy)
     fbuf[col, row] = features[:, pl.ds(pl.multiple_of(z * block, block), block)]
 
-    local = []
-    for index, weight in enumerate((weight_one, weight_two)):
+    def start_taps(index):
         copy = remote(
-            weight.at[:, :, :, lanes],
+            (weight_one, weight_two)[index].at[:, :, :, lanes],
             taps.at[index, :, :, mine, :],
             wx_send.at[index],
             wx_recv.at[index],
@@ -215,6 +214,11 @@
         )
         copy.start()
         pending.append(copy)
+
+    local = []
+    for index, weight in enumerate((weight_one, weight_two)):
+        if index == 0:
+            start_taps(0)
         copy = pltpu.make_async_copy(
             weight.at[:, :, :, lanes], taps.at[index, :, :, mine, :], local_sem.at[index]
         )
@@ -433,6 +437,7 @@
         return result + bias[:, here]
 
     partial_conv(0)
+    start_taps(1)
     turn_ring(1)
 
     hidden = reduced(0, bias_one).astype(bf16)

time: 55.9 us -> 51.8 us (0.927)
  Pallas kernels: 54 us -> 49.6 us
    pallas_call x1, Pallas kernels: 54 us -> 49.6 us  [fused(): pl.pallas_call(fused_kernel, out_shape=jax.ShapeDtypeStruct((2, width, ch...]
where the time goes in v2:
time: 51.8 us; the launch traced here: 51.3 us
  Pallas kernels  49.6 us (96%)
  local copies, waits for them, and re-layouts  1.67 us (3%)
    pallas_call x1, Pallas kernels, fused(): pl.pallas_call(fused_kernel, out_shape=jax.ShapeDtypeStruct((2, width, ch...  49.6 us
    unnamed x1, local copies, waits for them, and re-layouts  1.67 us

profile of v2, /device:TPU:1, one launch (start us, length us, event | category | flops | bytes accessed | tf_op | source)
XLA Modules:
  0.0 51.3 jit_solution(2153819840617920399)
XLA Ops:
  0.0 49.6 %shard_map.109 = bf16[2,128,512]{2,1,0:T(8,128)(2,1)} custom-call(bf16[64,512]{1,0:T(8,128)(2,1)} %bitcast.8, f32[1,512]{1,0:T(1,128)} %bitcast.9, f32[1,512]{1,0:T(1,128)} %bitcast.10, f32[1,512]{1,0:T(1,128)} %bitcast.11, f32[1,512]{1,0:T(1,128)} %bitcast.12, f32[1,512]{1,0:T(1,128)} %bitcast.13, f32[1,512]{1,0:T(1,128)} %bitcast.14, f32[1,512]{1,0:T(1,128)} %bitcast.15, ...), custom_call_target="tpu_custom_call" | custom-call | tf_op jit(solution)/shard_map/pallas_call | solution.py:678
  49.6 1.7 %copy.13 = bf16[2,128,512]{2,1,0:T(8,128)(2,1)} copy(bf16[2,128,512]{2,1,0:T(8,128)(2,1)} %shard_map.109) | data formatting | bytes 524288

commit v3 on v2

--- a/solution.py
+++ b/solution.py
@@ -186,10 +186,23 @@
     pl.semaphore_signal(
         barrier, inc=1, device_id={"img": 1 - img}, device_id_type=pl.DeviceIdType.MESH
     )
-    pl.semaphore_wait(barrier, 2 * rows)
-
     lanes = pl.ds(pl.multiple_of(col * outs, outs), outs)
     mine = pl.ds(pl.multiple_of(x * share, share), share)
+    local = []
+    for index, weight in enumerate((weight_one, weight_two)):
+        copy = pltpu.make_async_copy(
+            weight.at[:, :, :, lanes], taps.at[index, :, :, mine, :], local_sem.at[index]
+        )
+        copy.start()
+        local.append(copy)
+    copy = pltpu.make_async_copy(
+        weight_up.at[:, :, :, lanes],
+        gathered.at[:, :, pl.ds(pl.multiple_of(row * share, share), share), :],
+        local_sem.at[2],
+    )
+    copy.start()
+    local.append(copy)
+    pl.semaphore_wait(barrier, 2 * rows)
 
     def feature_copy(step):
         target = (row + step) % rows
@@ -215,23 +228,9 @@
         copy.start()
         pending.append(copy)
 
-    local = []
     for index, weight in enumerate((weight_one, weight_two)):
         if index == 0:
             start_taps(0)
-        copy = pltpu.make_async_copy(
-            weight.at[:, :, :, lanes], taps.at[index, :, :, mine, :], local_sem.at[index]
-        )
-        copy.start()
-        local.append(copy)
-    copy = pltpu.make_async_copy(
-        weight_up.at[:, :, :, lanes],
-        gathered.at[:, :, pl.ds(pl.multiple_of(row * share, share), share), :],
-        local_sem.at[2],
-    )
-    copy.start()
-    local.append(copy)
-
     place = z * (1 - x) + (rows - 1 - z) * x
     piece = share // 2
 

time: 51.8 us -> 51.8 us (level)
  no operation moved by 1% of the time
where the time goes in v3:
time: 51.8 us; the launch traced here: 51.3 us
  Pallas kernels  49.6 us (96%)
  local copies, waits for them, and re-layouts  1.67 us (3%)
    pallas_call x1, Pallas kernels, fused(): pl.pallas_call(fused_kernel, out_shape=jax.ShapeDtypeStruct((2, width, ch...  49.6 us
    unnamed x1, local copies, waits for them, and re-layouts  1.67 us

profile of v3, /device:TPU:1, one launch (start us, length us, event | category | flops | bytes accessed | tf_op | source)
XLA Modules:
  0.0 51.3 jit_solution(18312018081503737868)
XLA Ops:
  0.0 49.6 %shard_map.109 = bf16[2,128,512]{2,1,0:T(8,128)(2,1)} custom-call(bf16[64,512]{1,0:T(8,128)(2,1)} %bitcast.8, f32[1,512]{1,0:T(1,128)} %bitcast.9, f32[1,512]{1,0:T(1,128)} %bitcast.10, f32[1,512]{1,0:T(1,128)} %bitcast.11, f32[1,512]{1,0:T(1,128)} %bitcast.12, f32[1,512]{1,0:T(1,128)} %bitcast.13, f32[1,512]{1,0:T(1,128)} %bitcast.14, f32[1,512]{1,0:T(1,128)} %bitcast.15, ...), custom_call_target="tpu_custom_call" | custom-call | tf_op jit(solution)/shard_map/pallas_call | solution.py:677
  49.6 1.7 %copy.13 = bf16[2,128,512]{2,1,0:T(8,128)(2,1)} copy(bf16[2,128,512]{2,1,0:T(8,128)(2,1)} %shard_map.109) | data formatting | bytes 524288
